TPU v7x, 32 devices: a whole 2x2x4 slice. The times are simulated.
32 devices in a mesh: dp: 4 (over x, core), tensor: 8 (over z, y).
Axes of the slice: x: 2, y: 2, z: 4, core: 2. Of those that a mesh axis runs over, the one named last changes fastest.
Arguments:
- attn_ctx: bfloat16 [2048, 8192], P('dp', 'tensor'), may hold values from -6 to 6
- w_out: bfloat16 [8192, 8192], P('tensor'), may hold values from -0.09375 to 0.09375
- resid: bfloat16 [2048, 8192], P(('dp', 'tensor')), may hold values from -6 to 6
- teacher_gain: bfloat16 [8192], replicated, may hold values from 0.25 to 1.75
- dest_row: int32 [2048], replicated, may hold values from 0 to 2047, as said below
- student_in: bfloat16 [2048, 4096], P('dp', 'tensor'), may hold values from -6 to 6
- student_gain: bfloat16 [4096], replicated, may hold values from 0.25 to 1.75
- w_gate: bfloat16 [4096, 14336], P('dp', 'tensor'), may hold values from -0.09375 to 0.09375
- w_up: bfloat16 [4096, 14336], P('dp', 'tensor'), may hold values from -0.09375 to 0.09375
- w_down: bfloat16 [14336, 4096], P('tensor', 'dp'), may hold values from -0.0625 to 0.0625
- proj: bfloat16 [4096, 8192], P('dp', 'tensor'), may hold values from -0.09375 to 0.09375
Outputs:
- student_out: bfloat16 [2048, 4096], P('dp', 'tensor')
- row_loss: float32 [2048], P('dp')
- residue: float32 [2048, 8192], P('dp', 'tensor')
Inputs may be any that keep to these rules, and one draw needn't show every extreme that they name: A permutation of the rows; of the 64 rows i in one aligned block of teacher rows, at most 32 have dest_row[i] in any one tile of 512 student rows, and some tile receives exactly 32 of them.
All inputs are finite; a program needn't handle non-finite values.
Results may differ from a plain program's by a relative error of at most 0.012.
Values may be sent and summed in bfloat16 or wider, within the bound.
A program may use at most 192 MiB of HBM per device.

v0:
```python
import functools

import jax
import jax.numpy as jnp
from jax import lax
from jax.experimental import pallas as pl
from jax.experimental.pallas import tpu as pltpu
from jax.sharding import PartitionSpec as P

F32 = jnp.float32
BF16 = jnp.bfloat16
CORES = 2
MESH = pl.DeviceIdType.MESH
ANY = pl.BlockSpec(memory_space=pl.ANY)
VMEM = pl.BlockSpec(memory_space=pltpu.VMEM)
GRANT = 60 * 1024 * 1024


class Place:
    def __init__(self):
        self.n_dp = lax.axis_size("dp")
        self.n_t = lax.axis_size("tensor")
        self.n_x = self.n_dp // CORES
        self.n_y = self.n_x if self.n_t % self.n_x == 0 else 1
        self.n_z = self.n_t // self.n_y
        self.far = self.n_t // 2
        self.dp = lax.axis_index("dp")
        self.t = lax.axis_index("tensor")
        self.x = lax.div(self.dp, CORES)
        self.core = lax.rem(self.dp, CORES)
        self.spot = self.spot_of(self.t)
        self.sibling = self.x * CORES + 1 - self.core

    def spot_of(self, t):
        n_y, n_z = self.n_y, self.n_z
        if n_y == 1:
            return t
        z, y = lax.div(t, n_y), lax.rem(t, n_y)
        on = lax.div(y + n_y - 1, n_y)
        r = n_z - 1 - z
        i = y - 1 + lax.rem(r, 2) * (n_y - 2 * y)
        return (1 - on) * z + on * (n_z + r * (n_y - 1) + i)

    def at(self, offset):
        n_y, n_z = self.n_y, self.n_z
        p = lax.rem(self.spot + (offset + self.n_t), self.n_t)
        if n_y == 1:
            return p
        on = lax.div(lax.div(p, n_z) + n_y - 1, n_y)
        q = on * (p - n_z)
        r, i = lax.div(q, n_y - 1), lax.rem(q, n_y - 1)
        z = (1 - on) * p + on * (n_z - 1 - r)
        y = on * (1 + i + lax.rem(r, 2) * (n_y - 2 - 2 * i))
        return z * n_y + y

    def x_at(self, s):
        return lax.rem(self.x + s, self.n_x)

    def peer(self, s):
        return self.x_at(s) * CORES + self.core


def greet(devices):
    barrier = pltpu.get_barrier_semaphore()
    for device in devices:
        pl.semaphore_signal(barrier, inc=1, device_id=device, device_id_type=MESH)
    pl.semaphore_wait(barrier, len(devices))


def push(src, dst, send, recv, device):
    return pltpu.make_async_remote_copy(
        src_ref=src, dst_ref=dst, send_sem=send, recv_sem=recv, device_id=device, device_id_type=MESH
    )


def column_part(w, parts):
    cols = w.shape[1] // parts
    if cols % 128 == 0:
        return w
    return w.reshape(w.shape[0], parts, cols).transpose(1, 0, 2)


def part_of(ref, at, cols):
    if len(ref.shape) == 3:
        return ref.at[at]
    return ref.at[:, pl.ds(pl.multiple_of(at * cols, cols), cols)]


def gather_kernel(
    cols, rows_in, gate, up, down, x_all, gates, ups, downs,
    own_sem, ring_send, ring_recv, x_send, x_recv, core_send, core_recv,
):
    me = Place()
    n_x, far = me.n_x, me.far
    half = rows_in.shape[0] // 2
    line = [(me.dp, me.at(1)), (me.dp, me.at(-1))]
    peers = [(me.peer(s), me.t) for s in range(1, n_x)]
    twin = (me.sibling, me.t)
    greet(line + peers + [twin])

    own = pltpu.make_async_copy(rows_in, x_all.at[me.t, me.x], own_sem)
    own.start()

    def ring(k, d, s):
        t = me.at((1 - k) * (1 - 2 * d))
        dst = x_all.at[t, me.x_at(s)]
        src = rows_in if k == 1 and s == 0 else dst
        if k == far:
            rows = pl.ds(d * half, half)
            src, dst = src.at[rows], dst.at[rows]
        at = (d, k - 1, s)
        return push(src, dst, ring_send.at[at], ring_recv.at[at], line[d])

    started = []

    def start(copy):
        copy.start()
        started.append(copy)
        return copy

    hops = {}
    for d in range(2):
        hops[1, d, 0] = start(ring(1, d, 0))
    cross = [
        start(push(rows_in, x_all.at[me.t, me.x], x_send.at[0, s - 1], x_recv.at[0, s - 1], peers[s - 1]))
        for s in range(1, n_x)
    ]
    moved = {}
    for i, (w, buf) in enumerate(((gate, gates), (up, ups)), 1):
        for s in range(1, n_x):
            moved[i, s] = start(
                push(part_of(w, me.x_at(s), cols), buf.at[me.dp], x_send.at[i, s - 1], x_recv.at[i, s - 1], peers[s - 1])
            )
    twins = [
        start(push(part_of(gate, me.x, cols), gates.at[me.dp], core_send.at[0, 0], core_recv.at[0, 0], twin)),
        start(push(part_of(up, me.x, cols), ups.at[me.dp], core_send.at[1, 0], core_recv.at[1, 0], twin)),
        start(push(down, downs, core_send.at[2, 0], core_recv.at[2, 0], twin)),
    ]
    for s in range(1, n_x):
        cross[n_x - s - 1].wait_recv()
        for d in range(2):
            hops[1, d, s] = start(ring(1, d, s))

    def relay(i):
        buf = (gates, ups)[i - 1]
        for s in range(1, n_x):
            moved[i, s].wait_recv()
            block = buf.at[me.peer(n_x - s)]
            twins.append(start(push(block, block, core_send.at[i - 1, s], core_recv.at[i - 1, s], twin)))

    for k in range(1, far):
        for s in range(n_x):
            for d in range(2):
                hops[k, d, s].wait_recv()
                hops[k + 1, d, s] = start(ring(k + 1, d, s))
        if k == far - 2:
            relay(1)
    for s in range(n_x):
        for d in range(2):
            hops[far, d, s].wait_recv()
    if far < 3:
        relay(1)
    relay(2)
    for copy in twins:
        copy.wait_recv()
    own.wait()
    for copy in started:
        copy.wait_send()


def gather_rows(student_in, w_gate, w_up, w_down):
    n_dp, n_t = lax.axis_size("dp"), lax.axis_size("tensor")
    n_x = n_dp // CORES
    depth, cols = w_gate.shape[0], w_gate.shape[1] // n_x
    buf = jax.ShapeDtypeStruct((n_dp, depth, cols), BF16)
    sems = pltpu.SemaphoreType.DMA
    return pl.pallas_call(
        functools.partial(gather_kernel, cols),
        out_shape=(
            jax.ShapeDtypeStruct((n_t, n_x) + student_in.shape, BF16),
            buf,
            buf,
            jax.ShapeDtypeStruct(w_down.shape, BF16),
        ),
        in_specs=[VMEM, ANY, ANY, ANY],
        out_specs=(ANY,) * 4,
        scratch_shapes=[
            sems(()),
            sems((2, n_t // 2, n_x)),
            sems((2, n_t // 2, n_x)),
            sems((3, n_x)),
            sems((3, n_x)),
            sems((3, n_x)),
            sems((3, n_x)),
        ],
        compiler_params=pltpu.CompilerParams(collective_id=0, has_side_effects=True, vmem_limit_bytes=GRANT),
        name="gather_rows",
    )(student_in, column_part(w_gate, n_x), column_part(w_up, n_x), w_down)


def gated_kernel(cols, gain, x_all, gate, up, gates, ups, out, x_v, g_v, u_v, g_sum, u_sum, squares, x_sem, g_sem, u_sem):
    me = Place()
    n_x, n_dp, n_t = me.n_x, me.n_dp, me.n_t
    per = n_t // n_dp
    tokens, width = x_all.shape[2], x_all.shape[3]
    rows = n_x * tokens
    for i in range(n_dp):
        for own, buf, dst, sem in ((gate, gates, g_v, g_sem), (up, ups, u_v, u_sem)):

            @pl.when(me.dp == i)
            def _():
                pltpu.make_async_copy(part_of(own, me.x, cols), dst.at[i], sem.at[i]).start()

            @pl.when(me.dp != i)
            def _():
                pltpu.make_async_copy(buf.at[i], dst.at[i], sem.at[i]).start()

        for j in range(per):
            for x in range(n_x):
                pltpu.make_async_copy(
                    x_all.at[i * per + j, x],
                    x_v.at[i, pl.ds(x * tokens, tokens), pl.ds(j * width, width)],
                    x_sem.at[i, j, x],
                ).start()
    tile = min(256, rows)
    for i in range(n_dp):
        for j in range(per):
            for x in range(n_x):
                pltpu.make_async_copy(
                    x_all.at[i * per + j, x],
                    x_v.at[i, pl.ds(x * tokens, tokens), pl.ds(j * width, width)],
                    x_sem.at[i, j, x],
                ).wait()
        pltpu.make_async_copy(gates.at[i], g_v.at[i], g_sem.at[i]).wait()
        pltpu.make_async_copy(ups.at[i], u_v.at[i], u_sem.at[i]).wait()
        weight = gain[:, i * per * width : (i + 1) * per * width].astype(F32)

        @pl.loop(0, rows // tile)
        def _(r):
            at = pl.ds(pl.multiple_of(r * tile, tile), tile)
            x = x_v[i, at, :].astype(F32)
            square = jnp.sum(x * x, axis=1, keepdims=True)
            scaled = (x * weight).astype(BF16)
            g = jnp.dot(scaled, g_v[i], preferred_element_type=F32)
            u = jnp.dot(scaled, u_v[i], preferred_element_type=F32)
            if i:
                square = square + squares[at, :]
                g = g + g_sum[at, :]
                u = u + u_sum[at, :]
            if i < n_dp - 1:
                squares[at, :] = square
                g_sum[at, :] = g
                u_sum[at, :] = u
            else:
                scale = lax.rsqrt(square / (n_t * width) + 1e-05)
                g = g * scale
                out[at, :] = (jax.nn.silu(g) * (u * scale)).astype(BF16)


def gated(student_gain, x_all, w_gate, w_up, gates, ups):
    n_dp, depth, cols = gates.shape
    n_t, n_x, tokens, width = x_all.shape
    per = n_t // n_dp
    rows = n_x * tokens
    sems = pltpu.SemaphoreType.DMA
    flops = 4 * rows * n_dp * depth * cols
    return pl.pallas_call(
        functools.partial(gated_kernel, cols),
        out_shape=jax.ShapeDtypeStruct((rows, cols), BF16),
        in_specs=[VMEM] + [ANY] * 5,
        out_specs=VMEM,
        scratch_shapes=[
            pltpu.VMEM((n_dp, rows, per * width), BF16),
            pltpu.VMEM((n_dp, depth, cols), BF16),
            pltpu.VMEM((n_dp, depth, cols), BF16),
            pltpu.VMEM((rows, cols), F32),
            pltpu.VMEM((rows, cols), F32),
            pltpu.VMEM((rows, 1), F32),
            sems((n_dp, per, n_x)),
            sems((n_dp,)),
            sems((n_dp,)),
        ],
        compiler_params=pltpu.CompilerParams(vmem_limit_bytes=GRANT),
        cost_estimate=pl.CostEstimate(flops=flops, bytes_accessed=23_000_000, transcendentals=0),
        name="gated",
    )(student_gain[None, :], x_all, column_part(w_gate, n_x), column_part(w_up, n_x), gates, ups)


def as_row(column):
    return jnp.transpose(jnp.broadcast_to(column, (column.shape[0], 128)))[:8]


def as_column(row):
    return jnp.transpose(jnp.broadcast_to(row[:1], (128, row.shape[1])))[:, :1]


def add_over(peers, own, got, send, recv):
    copies = [push(own, got.at[k], send.at[k], recv.at[k], peer) for k, peer in enumerate(peers)]
    for copy in copies:
        copy.start()
    total = own[...]
    for k, copy in enumerate(copies):
        copy.wait_recv()
        total = total + got[k]
    for copy in copies:
        copy.wait_send()
    return total


def teacher_kernel(
    ctx, resid, gain, hidden, w_out, proj, out, hiddens, projs,
    w_v, sums, sent, got, total, row, rows_got,
    w_sem, send, recv, x_send, x_recv, core_send, core_recv, row_send, row_recv,
):
    me = Place()
    n_t, far = me.n_t, me.far
    width = w_v.shape[2]
    half = ctx.shape[0] // 2
    own = resid.shape[0]
    line = [(me.dp, me.at(1)), (me.dp, me.at(-1))]
    order = [far]
    for k in range(far - 1, 0, -1):
        order += [k, -k]
    order += [0]
    slot = {k: i for i, k in enumerate(order)}

    def load(k):
        cols = pl.ds(pl.multiple_of(me.at(k) * width, width), width)
        return pltpu.make_async_copy(w_out.at[:, cols], w_v.at[slot[k]], w_sem.at[slot[k]])

    for k in order:
        load(k).start()
    peers = [(me.peer(s), me.t) for s in range(1, me.n_x)]
    twin = (me.sibling, me.t)
    plane = [(me.dp, lax.rem(me.t + k, n_t)) for k in range(1, n_t)]
    greet(plane + peers + [twin])
    shared = []
    for s, peer in enumerate(peers):
        shared.append(push(hidden, hiddens.at[me.x], x_send.at[0, s], x_recv.at[0, s], peer))
    for s, peer in enumerate(peers):
        shared.append(push(proj, projs.at[me.dp], x_send.at[1, s], x_recv.at[1, s], peer))
    shared.append(push(proj, projs.at[me.dp], core_send.at[0], core_recv.at[0], twin))
    for copy in shared:
        copy.start()
    tile = min(256, width)

    def term(k, u):
        @pl.loop(0, width // tile)
        def _(c):
            cols = pl.ds(pl.multiple_of(c * tile, tile), tile)
            sums[:, cols] = jnp.dot(
                ctx[u * half : (u + 1) * half, :], w_v[slot[k], :, cols], preferred_element_type=F32
            )

        first = me.t * own

        @pl.when(lax.div(first, half) == u)
        def _():
            rows = pl.ds(pl.multiple_of(first - u * half, own), own)
            cols = pl.ds(pl.multiple_of(me.at(k) * width, width), width)
            sums[rows, :] = sums[rows, :] + resid[:, cols].astype(F32)

    def hop(k, d, u):
        at = (d, k - 1, u)
        return push(sent.at[at], got.at[at], send.at[at], recv.at[at], line[d])

    load(far).wait()
    for d in range(2):
        term(far, d)
        sent[d, far - 1, d] = sums[...].astype(BF16)
        hop(far, d, d).start()
    for k in range(far - 1, 0, -1):
        for d in range(2):
            load(k if d == 0 else -k).wait()
        for i in range(2):
            for d in range(2):
                u = (d + i + (k == far - 1)) % 2
                term(k if d == 0 else -k, u)
                if k + 1 < far or u == d:
                    hop(k + 1, d, u).wait_recv()
                    sent[d, k - 1, u] = (sums[...] + got[d, k, u].astype(F32)).astype(BF16)
                else:
                    sent[d, k - 1, u] = sums[...].astype(BF16)
                hop(k, d, u).start()
    load(0).wait()
    for i in range(2):
        term(0, i)
        for d in range(2):
            hop(1, d, i).wait_recv()
        total[i * half : (i + 1) * half, :] = (
            sums[...] + got[0, 0, i].astype(F32) + got[1, 0, i].astype(F32)
        )
    row[...] = as_row(jnp.sum(total[...] * total[...], axis=1, keepdims=True))
    for s in range(1, me.n_x):
        shared[me.n_x - 2 + s].wait_recv()
        block = projs.at[me.peer(me.n_x - s)]
        copy = push(block, block, core_send.at[s], core_recv.at[s], twin)
        copy.start()
        shared.append(copy)
    squares = add_over(plane, row, rows_got, row_send, row_recv)
    scale = as_column(lax.rsqrt(squares / (n_t * width) + 1e-06))
    weight = gain[:, pl.ds(pl.multiple_of(me.t * width, width), width)].astype(F32)
    out[...] = (total[...] * scale * weight).astype(BF16)
    for i, copy in enumerate(shared):
        if not me.n_x - 1 <= i < 2 * (me.n_x - 1):
            copy.wait_recv()
        copy.wait_send()
    for d in range(2):
        hop(far, d, d).wait_send()
        for k in range(far - 1, 0, -1):
            for u in range(2):
                hop(k, d, u).wait_send()


def teacher(attn_ctx, resid, w_out, teacher_gain, hidden, proj):
    n_t, n_dp = lax.axis_size("tensor"), lax.axis_size("dp")
    n_x = n_dp // CORES
    tokens, depth = attn_ctx.shape
    width = w_out.shape[1] // n_t
    sems = pltpu.SemaphoreType.DMA
    units = (2, n_t // 2, 2)
    return pl.pallas_call(
        teacher_kernel,
        out_shape=(
            jax.ShapeDtypeStruct((tokens, width), BF16),
            jax.ShapeDtypeStruct((n_x,) + hidden.shape, BF16),
            jax.ShapeDtypeStruct((n_dp,) + proj.shape, BF16),
        ),
        in_specs=[VMEM, VMEM, VMEM, ANY, ANY, ANY],
        out_specs=(VMEM, ANY, ANY),
        scratch_shapes=[
            pltpu.VMEM((n_t, depth, width), BF16),
            pltpu.VMEM((tokens // 2, width), F32),
            pltpu.VMEM(units + (tokens // 2, width), BF16),
            pltpu.VMEM(units + (tokens // 2, width), BF16),
            pltpu.VMEM((tokens, width), F32),
            pltpu.VMEM((8, tokens), F32),
            pltpu.VMEM((n_t - 1, 8, tokens), F32),
            sems((n_t,)),
            sems(units),
            sems(units),
            sems((2, n_x)),
            sems((2, n_x)),
            sems((n_x,)),
            sems((n_x,)),
            sems((n_t - 1,)),
            sems((n_t - 1,)),
        ],
        compiler_params=pltpu.CompilerParams(collective_id=1, has_side_effects=True, vmem_limit_bytes=GRANT),
        name="teacher",
    )(attn_ctx, resid, teacher_gain[None, :], hidden, w_out, proj)


def student_kernel(
    final, dest, hid_own, hiddens, w_down, downs, proj, projs, x_all, out, residue, loss,
    d_v, h_v, p_v, fin, full, mixed, here, sent, got, sums, target, column, row, rows_got,
    d_sem, h_sem, p_sem, here_sem, send, recv, fin_send, fin_recv, twin_send, twin_recv,
    swap_send, swap_recv, ring_send, ring_recv, row_send, row_recv,
):
    me = Place()
    n_x, n_t, n_dp, far = me.n_x, me.n_t, me.n_dp, me.far
    cols = h_v.shape[2]
    unit, block = d_v.shape[2], full.shape[3]
    tokens = final.shape[0]
    per = n_t // n_x
    half = sums.shape[0] // 2
    line = [(me.dp, me.at(1)), (me.dp, me.at(-1))]
    peers = [(me.peer(s), me.t) for s in range(1, n_x)]
    twin = (me.sibling, me.t)
    plane = [(me.dp, lax.rem(me.t + k, n_t)) for k in range(1, n_t)]

    def either(mine, index, own, other, dst, sem):
        @pl.when(mine == index)
        def _():
            pltpu.make_async_copy(own, dst, sem).start()

        @pl.when(mine != index)
        def _():
            pltpu.make_async_copy(other, dst, sem).start()

    for x in range(n_x):
        either(me.x, x, hid_own, hiddens.at[x], h_v.at[x], h_sem.at[x])
    for u in range(CORES):
        either(me.core, u, w_down, downs, d_v.at[u], d_sem.at[u])
    mine_rows = pl.ds(pl.multiple_of(me.t * block, block), block)
    width = x_all.shape[3]
    heres = [
        pltpu.make_async_copy(
            x_all.at[me.x * per + j, x, mine_rows], here.at[x, :, pl.ds(j * width, width)], here_sem.at[x, j]
        )
        for x in range(n_x)
        for j in range(per)
    ]
    for copy in heres:
        copy.start()
    for i in range(n_dp):
        either(me.dp, i, proj, projs.at[i], p_v.at[i], p_sem.at[i])
    greet(plane + peers + [twin])
    finals = [
        push(final, fin.at[me.dp], fin_send.at[s], fin_recv.at[s], peer) for s, peer in enumerate(peers)
    ] + [push(final, fin.at[me.dp], twin_send.at[0], twin_recv.at[0], twin)]
    for copy in finals:
        copy.start()
    fin[me.dp] = final[...]
    column[...] = jnp.zeros_like(column)
    for x in range(n_x):
        pltpu.make_async_copy(hid_own, h_v.at[x], h_sem.at[x]).wait()

    tile = min(256, unit)

    def term(k, u):
        t = me.at(k)

        @pl.loop(0, unit // tile)
        def _(c):
            at = pl.ds(pl.multiple_of(c * tile, tile), tile)
            total = None
            for x in range(n_x):
                rows = [h_v[x, pl.ds(pl.multiple_of(y * tokens + t * block, block), block), :] for y in range(n_x)]
                piece = jnp.dot(
                    jnp.concatenate(rows, axis=0),
                    d_v[u, x * cols : (x + 1) * cols, at],
                    preferred_element_type=F32,
                )
                total = piece if total is None else total + piece
            sums[:, at] = total

    def hop(k, d, u):
        at = (d, k - 1, u)
        src, dst = sent.at[at], got.at[at]
        if k == far:
            src, dst = src.at[pl.ds(d * half, half)], dst.at[pl.ds(d * half, half)]
        return push(src, dst, send.at[at], recv.at[at], line[d])

    for u in range(CORES):
        pltpu.make_async_copy(w_down, d_v.at[u], d_sem.at[u]).wait()
        term(far, u)
        for d in range(2):
            rows = slice(d * half, (d + 1) * half)
            sent[d, far - 1, u, rows] = sums[rows].astype(BF16)
            hop(far, d, u).start()
    for k in range(far - 1, 0, -1):
        for u in range(CORES):
            for d in range(2):
                term(k if d == 0 else -k, u)
                hop(k + 1, d, u).wait_recv()
                if k + 1 == far:
                    rows, rest = (slice(d * half, (d + 1) * half), slice((1 - d) * half, (2 - d) * half))
                    sent[d, k - 1, u, rows] = (sums[rows] + got[d, k, u, rows].astype(F32)).astype(BF16)
                    sent[d, k - 1, u, rest] = sums[rest].astype(BF16)
                else:
                    sent[d, k - 1, u] = (sums[...] + got[d, k, u].astype(F32)).astype(BF16)
                hop(k, d, u).start()
    for copy in heres:
        copy.wait()
    swaps = []
    for u in range(CORES):
        term(0, u)
        for d in range(2):
            hop(1, d, u).wait_recv()
        mlp = sums[...] + got[0, 0, u].astype(F32) + got[1, 0, u].astype(F32)
        known = here[:, :, u * unit : (u + 1) * unit].astype(F32)
        mixed[u] = (known + mlp.reshape(n_x, block, unit)).astype(BF16)
        full[me.t, u, me.x] = mixed[u, me.x]
        for s, peer in enumerate(peers):
            at = (u, s)
            copy = push(mixed.at[u, me.x_at(s + 1)], full.at[me.t, u, me.x], swap_send.at[at], swap_recv.at[at], peer)
            copy.start()
            swaps.append(copy)

    for s in range(1, n_x):
        finals[s - 1].wait_recv()
        piece = fin.at[me.peer(n_x - s)]
        copy = push(piece, piece, twin_send.at[s], twin_recv.at[s], twin)
        copy.start()
        finals.append(copy)

    def ring(k, d, u):
        t = me.at((1 - k) * (1 - 2 * d))
        view = full.at[t, u]
        if k == far:
            view = full.at[t, u, :, pl.ds(d * (block // 2), block // 2)]
        at = (d, k - 1, u)
        return push(view, view, ring_send.at[at], ring_recv.at[at], line[d])

    for u in range(CORES):
        for s in range(n_x - 1):
            swaps[u * (n_x - 1) + s].wait_recv()
        for d in range(2):
            ring(1, d, u).start()

    for copy in finals[n_x - 1 :]:
        copy.wait_recv()
    strip = min(256, tokens)

    @pl.loop(0, tokens // strip)
    def _(r):
        first = pl.multiple_of(r * strip, strip)
        places = me.dp * tokens + first + lax.broadcasted_iota(jnp.int32, (strip, tokens), 0)
        total = None
        for i in range(n_dp):
            pick = (places == dest[:, i * tokens : (i + 1) * tokens]).astype(F32).astype(BF16)
            piece = jnp.dot(pick, fin[i], preferred_element_type=F32)
            total = piece if total is None else total + piece
        target[pl.ds(first, strip), :] = total

    for i in range(n_dp):
        pltpu.make_async_copy(proj, p_v.at[i], p_sem.at[i]).wait()
    p_tile = min(256, target.shape[1])

    def project(ts):
        @pl.loop(0, target.shape[1] // p_tile)
        def _(c):
            at = pl.ds(pl.multiple_of(c * p_tile, p_tile), p_tile)
            total = None
            for x in range(n_x):
                for u in range(CORES):
                    rows = jnp.concatenate([full[t, u, x] for t in ts], axis=0)
                    piece = jnp.dot(rows, p_v[x * CORES + u, :, at], preferred_element_type=F32)
                    total = piece if total is None else total + piece
            for i, t in enumerate(ts):
                rows = pl.ds(pl.multiple_of(t * block, block), block)
                gap = total[i * block : (i + 1) * block] - target[rows, at]
                residue[rows, at] = gap
                column[rows, :] = column[rows, :] + jnp.sum(gap * gap, axis=1, keepdims=True)

    project([me.t])
    for k in range(1, far + 1):
        for u in range(CORES):
            for d in range(2):
                ring(k, d, u).wait_recv()
                if k < far:
                    ring(k + 1, d, u).start()
        project([me.at(-k), me.at(k)] if k < far else [me.at(far)])

    row[...] = as_row(column[...])
    out_cols = out.shape[1]
    x = lax.div(me.t, per)
    u = lax.div(lax.rem(me.t, per) * out_cols, unit)
    inner = pl.multiple_of(lax.rem(me.t * out_cols, unit), out_cols)
    for t in range(n_t):
        out[t * block : (t + 1) * block, :] = full[t, u, x, :, pl.ds(inner, out_cols)]
    loss[...] = add_over(plane, row, rows_got, row_send, row_recv) / (n_t * target.shape[1])
    for u in range(CORES):
        for d in range(2):
            for k in range(1, far + 1):
                hop(k, d, u).wait_send()
                ring(k, d, u).wait_send()
    for copy in finals + swaps:
        copy.wait_send()


def student(final, dest_row, hidden, hiddens, w_down, downs, proj, projs, x_all):
    n_t, n_dp = lax.axis_size("tensor"), lax.axis_size("dp")
    n_x, far = n_dp // CORES, n_t // 2
    tokens, width = final.shape
    ff, unit = w_down.shape
    rows, cols = hidden.shape
    block = tokens // n_t
    d_cols = x_all.shape[3]
    sems = pltpu.SemaphoreType.DMA
    hops = (2, far, CORES)
    vmem = pltpu.VMEM
    return pl.pallas_call(
        student_kernel,
        out_shape=(
            jax.ShapeDtypeStruct((tokens, d_cols), BF16),
            jax.ShapeDtypeStruct((tokens, width), F32),
            jax.ShapeDtypeStruct((8, tokens), F32),
        ),
        in_specs=[VMEM, VMEM] + [ANY] * 7,
        out_specs=(VMEM, VMEM, VMEM),
        scratch_shapes=[
            vmem((CORES, ff, unit), BF16),
            vmem((n_x, rows, cols), BF16),
            vmem((n_dp,) + proj.shape, BF16),
            vmem((n_dp, tokens, width), BF16),
            vmem((n_t, CORES, n_x, block, unit), BF16),
            vmem((CORES, n_x, block, unit), BF16),
            vmem((n_x, block, CORES * unit), BF16),
            vmem(hops + (n_x * block, unit), BF16),
            vmem(hops + (n_x * block, unit), BF16),
            vmem((n_x * block, unit), F32),
            vmem((tokens, width), F32),
            vmem((tokens, 1), F32),
            vmem((8, tokens), F32),
            vmem((n_t - 1, 8, tokens), F32),
            sems((CORES,)),
            sems((n_x,)),
            sems((n_dp,)),
            sems((n_x, n_t // n_x)),
            sems(hops),
            sems(hops),
            sems((n_x,)),
            sems((n_x,)),
            sems((n_x,)),
            sems((n_x,)),
            sems((CORES, n_x)),
            sems((CORES, n_x)),
            sems(hops),
            sems(hops),
            sems((n_t - 1,)),
            sems((n_t - 1,)),
        ],
        compiler_params=pltpu.CompilerParams(collective_id=2, has_side_effects=True, vmem_limit_bytes=GRANT),
        name="student",
    )(final, dest_row[None, :], hidden, hiddens, w_down, downs, proj, projs, x_all)


def local(
    attn_ctx,
    w_out,
    resid,
    teacher_gain,
    dest_row,
    student_in,
    student_gain,
    w_gate,
    w_up,
    w_down,
    proj,
):
    x_all, gates, ups, downs = gather_rows(student_in, w_gate, w_up, w_down)
    hidden = gated(student_gain, x_all, w_gate, w_up, gates, ups)
    final, hiddens, projs = teacher(attn_ctx, resid, w_out, teacher_gain, hidden, proj)
    out, residue, loss = student(final, dest_row, hidden, hiddens, w_down, downs, proj, projs, x_all)
    return (out, loss[0], residue)


def solution(mesh):
    placed = (
        P("dp", "tensor"),
        P("tensor", None),
        P(("dp", "tensor"), None),
        P(),
        P(),
        P("dp", "tensor"),
        P(),
        P("dp", "tensor"),
        P("dp", "tensor"),
        P("tensor", "dp"),
        P("dp", "tensor"),
    )
    return jax.shard_map(
        local,
        mesh=mesh,
        in_specs=placed,
        out_specs=(P("dp", "tensor"), P("dp"), P("dp", "tensor")),
        check_vma=False,
    )
```

profile of v0, /device:TPU:0, one launch (start us, length us, event | category | flops | bytes accessed | tf_op | source)
XLA Modules:
  0.0 335.4 jit_solution(3759212147879606944)
XLA Ops:
  0.6 1.3 broadcast_in_dim.10.gain
  1.9 1.3 broadcast_in_dim.9.gain
  3.3 100.2 %gather_rows.1 = (bf16[8,2,512,512]{3,2,1,0:T(8,128)(2,1)}, bf16[4,1024,896]{2,1,0:T(8,128)(2,1)}, bf16[4,1024,896]{2,1,0:T(8,128)(2,1)}, bf16[1792,1024]{1,0:T(8,128)(2,1)}) custom-call(bf16[512,512]{1,0:T(8,128)(2,1)} %rows_in.1, bf16[1024,1792]{1,0:T(8,128)(2,1)} %gate.3, bf16[1024,1792]{1,0:T(8,128)(2,1)} %up.3, bf16[1792,1024]{1,0:T(8,128)(2,1)} %w_down.1), custom_call_target="tpu_custom_call" | custom-call | tf_op jit(solution)/shard_map/gather_rows/pallas_call | solution.py:177
  103.5 26.3 %gated.1.hidden.hid_own = bf16[1024,896]{1,0:T(8,128)(2,1)} custom-call(bf16[1,4096]{1,0:T(2,128)(2,1)} %broadcast_in_dim.10.gain, bf16[8,2,512,512]{3,2,1,0:T(8,128)(2,1)} %get-tuple-element.13.x_all, bf16[1024,1792]{1,0:T(8,128)(2,1)} %gate.3, bf16[1024,1792]{1,0:T(8,128)(2,1)} %up.3, bf16[4,1024,896]{2,1,0:T(8,128)(2,1)} %get-tuple-element.14.gates, ...), custom_call_target="tpu_custom_call" | custom-call | flops 15032385536 | bytes 23000000 | tf_op jit(solution)/shard_map/gated/pallas_call | solution.py:267
  129.8 98.4 %teacher.1 = (bf16[512,1024]{1,0:T(8,128)(2,1)}, bf16[2,1024,896]{2,1,0:T(8,128)(2,1)}, bf16[4,1024,1024]{2,1,0:T(8,128)(2,1)}) custom-call(bf16[512,1024]{1,0:T(8,128)(2,1)} %ctx.1, bf16[64,8192]{1,0:T(8,128)(2,1)} %resid.1, bf16[1,8192]{1,0:T(2,128)(2,1)} %broadcast_in_dim.9.gain, bf16[1024,896]{1,0:T(8,128)(2,1)} %gated.1.hidden.hid_own, ...), custom_call_target="tpu_custom_call" | custom-call | tf_op jit(solution)/shard_map/teacher/pallas_call | solution.py:422
  228.2 100.8 %student.1 = (bf16[512,512]{1,0:T(8,128)(2,1)}, f32[512,1024]{1,0:T(8,128)}, f32[8,512]{1,0:T(8,128)}) custom-call(bf16[512,1024]{1,0:T(8,128)(2,1)} %get-tuple-element.16.final, s32[1,2048]{1,0:T(1,128)} %bitcast.2, bf16[1024,896]{1,0:T(8,128)(2,1)} %gated.1.hidden.hid_own, bf16[2,1024,896]{2,1,0:T(8,128)(2,1)} %get-tuple-element.17.hiddens, ...), custom_call_target="tpu_custom_call" | custom-call | tf_op jit(solution)/shard_map/student/pallas_call | solution.py:664
  329.1 1.3 slice.3
  330.4 1.9 copy.16
  332.2 3.2 copy.17
where the time goes:
time: 336 us; the launch traced here: 335 us
  Pallas kernels  326 us (97%)
  local copies, waits for them, and re-layouts  8.97 us (3%)
    pallas_call x1, Pallas kernels, student(): pl.pallas_call(student_kernel, out_shape=(jax.ShapeDtypeStruct((tokens, d...  101 us
    pallas_call x1, Pallas kernels, gather_rows(): pl.pallas_call(functools.partial(gather_kernel, cols), out_shape=(jax.Sha...  100 us
    pallas_call x1, Pallas kernels, teacher(): pl.pallas_call(teacher_kernel, out_shape=(jax.ShapeDtypeStruct((tokens, w...  98.4 us
    pallas_call x1, Pallas kernels, gated(): pl.pallas_call(functools.partial(gated_kernel, cols), out_shape=jax.Shape...  26.3 us

commit v1 on v0

v1 whole, which is shorter than its diff:
```python
import functools

import jax
import jax.numpy as jnp
from jax import lax
from jax.experimental import pallas as pl
from jax.experimental.pallas import tpu as pltpu
from jax.sharding import PartitionSpec as P

F32 = jnp.float32
BF16 = jnp.bfloat16
CORES = 2
MESH = pl.DeviceIdType.MESH
ANY = pl.BlockSpec(memory_space=pl.ANY)
VMEM = pl.BlockSpec(memory_space=pltpu.VMEM)
GRANT = 62 * 1024 * 1024


class Place:
    def __init__(self):
        self.n_dp = lax.axis_size("dp")
        self.n_t = lax.axis_size("tensor")
        self.n_x = self.n_dp // CORES
        self.n_y = self.n_x if self.n_t % self.n_x == 0 else 1
        self.n_z = self.n_t // self.n_y
        self.far = self.n_t // 2
        self.dp = lax.axis_index("dp")
        self.t = lax.axis_index("tensor")
        self.x = lax.div(self.dp, CORES)
        self.core = lax.rem(self.dp, CORES)
        self.spot = self.spot_of(self.t)
        self.sibling = self.x * CORES + 1 - self.core

    def spot_of(self, t):
        n_y, n_z = self.n_y, self.n_z
        if n_y == 1:
            return t
        z, y = lax.div(t, n_y), lax.rem(t, n_y)
        on = lax.div(y + n_y - 1, n_y)
        r = n_z - 1 - z
        i = y - 1 + lax.rem(r, 2) * (n_y - 2 * y)
        return (1 - on) * z + on * (n_z + r * (n_y - 1) + i)

    def at(self, offset):
        n_y, n_z = self.n_y, self.n_z
        p = lax.rem(self.spot + (offset + self.n_t), self.n_t)
        if n_y == 1:
            return p
        on = lax.div(lax.div(p, n_z) + n_y - 1, n_y)
        q = on * (p - n_z)
        r, i = lax.div(q, n_y - 1), lax.rem(q, n_y - 1)
        z = (1 - on) * p + on * (n_z - 1 - r)
        y = on * (1 + i + lax.rem(r, 2) * (n_y - 2 - 2 * i))
        return z * n_y + y

    def x_at(self, s):
        return lax.rem(self.x + s, self.n_x)

    def peer(self, s):
        return self.x_at(s) * CORES + self.core


def greet(devices):
    barrier = pltpu.get_barrier_semaphore()
    for device in devices:
        pl.semaphore_signal(barrier, inc=1, device_id=device, device_id_type=MESH)
    pl.semaphore_wait(barrier, len(devices))


def push(src, dst, send, recv, device):
    return pltpu.make_async_remote_copy(
        src_ref=src, dst_ref=dst, send_sem=send, recv_sem=recv, device_id=device, device_id_type=MESH
    )


def column_part(w, parts):
    cols = w.shape[1] // parts
    if cols % 128 == 0:
        return w
    return w.reshape(w.shape[0], parts, cols).transpose(1, 0, 2)


def part_of(ref, at, cols):
    if len(ref.shape) == 3:
        return ref.at[at]
    return ref.at[:, pl.ds(pl.multiple_of(at * cols, cols), cols)]


def as_row(column):
    return jnp.transpose(jnp.broadcast_to(column, (column.shape[0], 128)))[:8]


def as_column(row):
    return jnp.transpose(jnp.broadcast_to(row[:1], (128, row.shape[1])))[:, :1]


def add_over(peers, own, got, send, recv):
    copies = [push(own, got.at[k], send.at[k], recv.at[k], peer) for k, peer in enumerate(peers)]
    for copy in copies:
        copy.start()
    total = own[...]
    for k, copy in enumerate(copies):
        copy.wait_recv()
        total = total + got[k]
    for copy in copies:
        copy.wait_send()
    return total


SLOTS = 4


def front_kernel(
    rows_in, s_gain, ctx, resid, t_gain, gate, up, down, w_out, proj,
    out, hiddens, projs, downs, here,
    x_v, g_v, u_v, g_sum, u_sum, squares, hid_v,
    w_v, sums, sent, got, total, row, rows_got,
    own_sem, ring_send, ring_recv, x_send, x_recv, core_send, core_recv,
    hid_send, hid_recv, w_sem, send, recv, row_send, row_recv,
):
    me = Place()
    n_x, n_t, n_dp, far = me.n_x, me.n_t, me.n_dp, me.far
    tokens, d_cols = rows_in.shape
    cols = g_v.shape[2]
    width = w_v.shape[2]
    half = tokens // 2
    own_rows = resid.shape[0]
    line = [(me.dp, me.at(1)), (me.dp, me.at(-1))]
    peers = [(me.peer(s), me.t) for s in range(1, n_x)]
    twin = (me.sibling, me.t)
    plane = [(me.dp, lax.rem(me.t + k, n_t)) for k in range(1, n_t)]

    order = [far]
    for k in range(far - 1, 0, -1):
        order += [k, -k]
    order += [0]
    slot = {k: i % SLOTS for i, k in enumerate(order)}

    def load(k):
        at = pl.ds(pl.multiple_of(me.at(k) * width, width), width)
        return pltpu.make_async_copy(w_out.at[:, at], w_v.at[slot[k]], w_sem.at[slot[k]])

    def reload(k):
        after = order.index(k) + SLOTS
        if after < len(order):
            load(order[after]).start()

    greet(plane + peers + [twin])
    started = []

    def start(copy):
        copy.start()
        started.append(copy)
        return copy

    def ring(k, d, s):
        t = me.at((1 - k) * (1 - 2 * d))
        dst = x_v.at[t, me.x_at(s)]
        src = rows_in if k == 1 and s == 0 else dst
        if k == far:
            at = pl.ds(d * half, half)
            src, dst = src.at[at], dst.at[at]
        at = (d, k - 1, s)
        return push(src, dst, ring_send.at[at], ring_recv.at[at], line[d])

    hops = {}
    for d in range(2):
        hops[1, d, 0] = start(ring(1, d, 0))
    cross = [
        start(push(rows_in, x_v.at[me.t, me.x], x_send.at[0, s], x_recv.at[0, s], peer))
        for s, peer in enumerate(peers)
    ]
    moved = {}
    for i, (w, buf) in enumerate(((gate, g_v), (up, u_v)), 1):
        for s, peer in enumerate(peers):
            moved[i, s] = start(
                push(part_of(w, me.x_at(s + 1), cols), buf.at[me.dp], x_send.at[i, s], x_recv.at[i, s], peer)
            )
    for s, peer in enumerate(peers):
        first = pl.ds(0, proj.shape[0] // 2)
        moved[3, s] = start(
            push(proj.at[first], projs.at[me.dp, first], x_send.at[3, s], x_recv.at[3, s], peer)
        )
    for o in range(min(SLOTS, len(order))):
        load(order[o]).start()
    owns = [
        pltpu.make_async_copy(rows_in, x_v.at[me.t, me.x], own_sem.at[0]),
        pltpu.make_async_copy(part_of(gate, me.x, cols), g_v.at[me.dp], own_sem.at[1]),
        pltpu.make_async_copy(part_of(up, me.x, cols), u_v.at[me.dp], own_sem.at[2]),
    ]
    for copy in owns:
        copy.start()
    early = [
        start(push(part_of(gate, me.x, cols), g_v.at[me.dp], core_send.at[0, 0], core_recv.at[0, 0], twin)),
        start(push(part_of(up, me.x, cols), u_v.at[me.dp], core_send.at[1, 0], core_recv.at[1, 0], twin)),
    ]
    late = [
        start(push(down, downs, core_send.at[2, 0], core_recv.at[2, 0], twin)),
        start(push(proj, projs.at[me.dp], core_send.at[3, 0], core_recv.at[3, 0], twin)),
    ]

    def relay(i, buf, copies):
        for s in range(1, n_x):
            moved[i, s - 1].wait_recv()
            block = buf.at[me.peer(n_x - s)]
            if i == 3:
                block = buf.at[me.peer(n_x - s), pl.ds(0, proj.shape[0] // 2)]
            at = (i if i == 3 else i - 1, s)
            copies.append(start(push(block, block, core_send.at[at], core_recv.at[at], twin)))

    for s in range(1, n_x):
        cross[n_x - s - 1].wait_recv()
        for d in range(2):
            hops[1, d, s] = start(ring(1, d, s))
    for k in range(1, far):
        for s in range(n_x):
            for d in range(2):
                hops[k, d, s].wait_recv()
                hops[k + 1, d, s] = start(ring(k + 1, d, s))
        if k == max(far - 2, 1):
            relay(1, g_v, early)

    tile = min(256, width)

    def term(k, u):
        @pl.loop(0, width // tile)
        def _(c):
            at = pl.ds(pl.multiple_of(c * tile, tile), tile)
            sums[:, at] = jnp.dot(
                ctx[u * half : (u + 1) * half, :], w_v[slot[k], :, at], preferred_element_type=F32
            )

        first = me.t * own_rows

        @pl.when(lax.div(first, half) == u)
        def _():
            rows = pl.ds(pl.multiple_of(first - u * half, own_rows), own_rows)
            at = pl.ds(pl.multiple_of(me.at(k) * width, width), width)
            sums[rows, :] = sums[rows, :] + resid[:, at].astype(F32)

    def hop(k, d, u):
        at = (d, k - 1, u)
        return push(sent.at[at], got.at[at], send.at[at], recv.at[at], line[d])

    load(far).wait()
    for d in range(2):
        term(far, d)
        sent[d, far - 1, d] = sums[...].astype(BF16)
        hop(far, d, d).start()
    reload(far)

    for s in range(n_x):
        for d in range(2):
            hops[far, d, s].wait_recv()
    for copy in owns:
        copy.wait()
    block = here.shape[1]
    per = n_t // n_x
    mine = pl.ds(pl.multiple_of(me.t * block, block), block)
    heres = [
        pltpu.make_async_copy(
            x_v.at[me.x * per + j, x, mine], here.at[x, :, pl.ds(j * d_cols, d_cols)], own_sem.at[3 + x * per + j]
        )
        for x in range(n_x)
        for j in range(per)
    ]
    for copy in heres:
        copy.start()

    strip = min(256, tokens)
    per_dp = n_t // n_dp
    strips = n_x * tokens // strip
    hid = []

    def gated(r):
        x, first = r * strip // tokens, r * strip % tokens

        @pl.loop(0, n_dp)
        def _(i):
            parts = [x_v[i * per_dp + j, x, first : first + strip, :] for j in range(per_dp)]
            rows = jnp.concatenate(parts, axis=1).astype(F32)
            depth = per_dp * d_cols
            weight = s_gain[:, pl.ds(pl.multiple_of(i * depth, depth), depth)].astype(F32)
            scaled = (rows * weight).astype(BF16)
            square = jnp.sum(rows * rows, axis=1, keepdims=True)
            g = jnp.dot(scaled, g_v[i], preferred_element_type=F32)
            u = jnp.dot(scaled, u_v[i], preferred_element_type=F32)

            @pl.when(i == 0)
            def _():
                squares[...] = square
                g_sum[...] = g
                u_sum[...] = u

            @pl.when(i > 0)
            def _():
                squares[...] = squares[...] + square
                g_sum[...] = g_sum[...] + g
                u_sum[...] = u_sum[...] + u

        scale = lax.rsqrt(squares[...] / (n_t * d_cols) + 1e-05)
        g = g_sum[...] * scale
        hid_v[r * strip : (r + 1) * strip, :] = (jax.nn.silu(g) * (u_sum[...] * scale)).astype(BF16)
        at = pl.ds(r * strip, strip)
        copy = pltpu.make_async_copy(hid_v.at[at], hiddens.at[me.x, at], hid_send.at[r, n_x - 1])
        copy.start()
        hid.append(copy)
        for s, peer in enumerate(peers):
            start(push(hid_v.at[at], hiddens.at[me.x, at], hid_send.at[r, s], hid_recv.at[r, s], peer))

    left = list(range(strips))
    turns = [(k, i) for k in range(far - 1, 0, -1) for i in range(2)][1:5]
    for k in range(far - 1, 0, -1):
        for d in range(2):
            load(k if d == 0 else -k).wait()
        for i in range(2):
            for d in range(2):
                u = (d + i + (k == far - 1)) % 2
                term(k if d == 0 else -k, u)
                if k + 1 < far or u == d:
                    hop(k + 1, d, u).wait_recv()
                    sent[d, k - 1, u] = (sums[...] + got[d, k, u].astype(F32)).astype(BF16)
                else:
                    sent[d, k - 1, u] = sums[...].astype(BF16)
                hop(k, d, u).start()
            if k == far - 1 and i == 1:
                relay(2, u_v, early)
                for copy in early:
                    copy.wait_recv()
            if (k, i) in turns:
                for _ in range(-(-strips // len(turns))):
                    if left:
                        gated(left.pop(0))
        reload(k)
        reload(-k)
    while left:
        gated(left.pop(0))
    load(0).wait()
    for i in range(2):
        term(0, i)
        for d in range(2):
            hop(1, d, i).wait_recv()
        total[i * half : (i + 1) * half, :] = (
            sums[...] + got[0, 0, i].astype(F32) + got[1, 0, i].astype(F32)
        )
    row[...] = as_row(jnp.sum(total[...] * total[...], axis=1, keepdims=True))
    relay(3, projs, late)
    sums_of = add_over(plane, row, rows_got, row_send, row_recv)
    scale = as_column(lax.rsqrt(sums_of / (n_t * width) + 1e-06))
    weight = t_gain[:, pl.ds(pl.multiple_of(me.t * width, width), width)].astype(F32)
    out[...] = (total[...] * scale * weight).astype(BF16)
    for copy in late:
        copy.wait_recv()
    for r in range(strips):
        at = pl.ds(r * strip, strip)
        for s, peer in enumerate(peers):
            push(hid_v.at[at], hiddens.at[me.x, at], hid_send.at[r, s], hid_recv.at[r, s], peer).wait_recv()
    for copy in hid + heres:
        copy.wait()
    for copy in started:
        copy.wait_send()
    for d in range(2):
        hop(far, d, d).wait_send()
        for k in range(far - 1, 0, -1):
            for u in range(2):
                hop(k, d, u).wait_send()


def front(student_in, student_gain, attn_ctx, resid, teacher_gain, w_gate, w_up, w_down, w_out, proj):
    n_t, n_dp = lax.axis_size("tensor"), lax.axis_size("dp")
    n_x, far = n_dp // CORES, n_t // 2
    tokens, d_cols = student_in.shape
    ctx_depth = attn_ctx.shape[1]
    width = w_out.shape[1] // n_t
    depth, cols = w_gate.shape[0], w_gate.shape[1] // n_x
    strip = min(256, tokens)
    strips = n_x * tokens // strip
    block, per = tokens // n_t, n_t // n_x
    sems, vmem = pltpu.SemaphoreType.DMA, pltpu.VMEM
    units = (2, far, 2)
    shape = jax.ShapeDtypeStruct
    return pl.pallas_call(
        front_kernel,
        out_shape=(
            shape((tokens, width), BF16),
            shape((n_x, n_x * tokens, cols), BF16),
            shape((n_dp,) + proj.shape, BF16),
            shape(w_down.shape, BF16),
            shape((n_x, block, per * d_cols), BF16),
        ),
        in_specs=[VMEM] * 5 + [ANY] * 5,
        out_specs=(VMEM, ANY, ANY, ANY, ANY),
        scratch_shapes=[
            vmem((n_t, n_x, tokens, d_cols), BF16),
            vmem((n_dp, depth, cols), BF16),
            vmem((n_dp, depth, cols), BF16),
            vmem((strip, cols), F32),
            vmem((strip, cols), F32),
            vmem((strip, 1), F32),
            vmem((n_x * tokens, cols), BF16),
            vmem((SLOTS, ctx_depth, width), BF16),
            vmem((tokens // 2, width), F32),
            vmem(units + (tokens // 2, width), BF16),
            vmem(units + (tokens // 2, width), BF16),
            vmem((tokens, width), F32),
            vmem((8, tokens), F32),
            vmem((n_t - 1, 8, tokens), F32),
            sems((3 + n_x * per,)),
            sems((2, far, n_x)),
            sems((2, far, n_x)),
            sems((4, n_x)),
            sems((4, n_x)),
            sems((4, n_x)),
            sems((4, n_x)),
            sems((strips, n_x)),
            sems((strips, n_x)),
            sems((SLOTS,)),
            sems(units),
            sems(units),
            sems((n_t - 1,)),
            sems((n_t - 1,)),
        ],
        compiler_params=pltpu.CompilerParams(collective_id=0, has_side_effects=True, vmem_limit_bytes=GRANT),
        name="front",
    )(
        student_in, student_gain[None, :], attn_ctx, resid, teacher_gain[None, :],
        column_part(w_gate, n_x), column_part(w_up, n_x), w_down, w_out, proj,
    )


def student_kernel(
    final, dest, here, hiddens, w_down, downs, proj, projs, out, residue, loss,
    d_v, h_v, p_v, fin, full, mixed, sent, got, sums, target, column, row, rows_got,
    d_sem, h_sem, p_sem, send, recv, fin_send, fin_recv, twin_send, twin_recv,
    swap_send, swap_recv, ring_send, ring_recv, row_send, row_recv, rest_send, rest_recv, kin_send, kin_recv,
):
    me = Place()
    n_x, n_t, n_dp, far = me.n_x, me.n_t, me.n_dp, me.far
    cols = h_v.shape[2]
    unit, block = d_v.shape[2], full.shape[3]
    tokens = final.shape[0]
    per = n_t // n_x
    half = sums.shape[1] // 2
    line = [(me.dp, me.at(1)), (me.dp, me.at(-1))]
    peers = [(me.peer(s), me.t) for s in range(1, n_x)]
    twin = (me.sibling, me.t)
    plane = [(me.dp, lax.rem(me.t + k, n_t)) for k in range(1, n_t)]

    def either(mine, index, own, other, dst, sem):
        @pl.when(mine == index)
        def _():
            pltpu.make_async_copy(own, dst, sem).start()

        @pl.when(mine != index)
        def _():
            pltpu.make_async_copy(other, dst, sem).start()

    for x in range(n_x):
        pltpu.make_async_copy(hiddens.at[x], h_v.at[x], h_sem.at[x]).start()
    for u in range(CORES):
        either(me.core, u, w_down, downs, d_v.at[u], d_sem.at[u])
    greet(plane + peers + [twin])
    finals = [
        push(final, fin.at[me.dp], fin_send.at[s], fin_recv.at[s], peer) for s, peer in enumerate(peers)
    ] + [push(final, fin.at[me.dp], twin_send.at[0], twin_recv.at[0], twin)]
    for copy in finals:
        copy.start()
    p_half = proj.shape[0] // 2
    second = pl.ds(p_half, p_half)
    rest_p = [
        push(proj.at[second], p_v.at[me.dp, second], rest_send.at[s], rest_recv.at[s], peer)
        for s, peer in enumerate(peers)
    ]
    for copy in rest_p:
        copy.start()
    fin[me.dp] = final[...]
    column[...] = jnp.zeros_like(column)
    for x in range(n_x):
        pltpu.make_async_copy(hiddens.at[x], h_v.at[x], h_sem.at[x]).wait()

    tile = min(256, unit)

    def term(ks, u):
        spots = [me.at(k) for k in ks]

        @pl.loop(0, unit // tile)
        def _(c):
            at = pl.ds(pl.multiple_of(c * tile, tile), tile)
            total = None
            for x in range(n_x):
                rows = [
                    h_v[x, pl.ds(pl.multiple_of(y * tokens + t * block, block), block), :]
                    for t in spots
                    for y in range(n_x)
                ]
                piece = jnp.dot(
                    jnp.concatenate(rows, axis=0),
                    d_v[u, x * cols : (x + 1) * cols, at],
                    preferred_element_type=F32,
                )
                total = piece if total is None else total + piece
            for i in range(len(ks)):
                sums[i, :, at] = total[i * 2 * half : (i + 1) * 2 * half]

    def hop(k, d, u):
        at = (d, k - 1, u)
        src, dst = sent.at[at], got.at[at]
        if k == far:
            src, dst = src.at[pl.ds(d * half, half)], dst.at[pl.ds(d * half, half)]
        return push(src, dst, send.at[at], recv.at[at], line[d])

    for u in range(CORES):
        pltpu.make_async_copy(w_down, d_v.at[u], d_sem.at[u]).wait()
        term([far], u)
        for d in range(2):
            rows = slice(d * half, (d + 1) * half)
            sent[d, far - 1, u, rows] = sums[0, rows].astype(BF16)
            hop(far, d, u).start()

    def of_proj(i, j, act):
        at = pl.ds(j * p_half, p_half)

        @pl.when(me.dp == i)
        def _():
            act(pltpu.make_async_copy(proj.at[at], p_v.at[i, at], p_sem.at[i, j]))

        @pl.when(me.dp != i)
        def _():
            act(pltpu.make_async_copy(projs.at[i, at], p_v.at[i, at], p_sem.at[i, j]))

    def all_proj(act):
        for i in range(n_dp):
            of_proj(i, 0, act)

            @pl.when(me.x == i // CORES)
            def _():
                of_proj(i, 1, act)

    all_proj(lambda copy: copy.start())
    for k in range(far - 1, 0, -1):
        for u in range(CORES):
            term([k, -k], u)
            for d in range(2):
                hop(k + 1, d, u).wait_recv()
                if k + 1 == far:
                    rows, rest = (slice(d * half, (d + 1) * half), slice((1 - d) * half, (2 - d) * half))
                    sent[d, k - 1, u, rows] = (sums[d, rows] + got[d, k, u, rows].astype(F32)).astype(BF16)
                    sent[d, k - 1, u, rest] = sums[d, rest].astype(BF16)
                else:
                    sent[d, k - 1, u] = (sums[d] + got[d, k, u].astype(F32)).astype(BF16)
                hop(k, d, u).start()
    swaps = []
    for u in range(CORES):
        term([0], u)
        for d in range(2):
            hop(1, d, u).wait_recv()
        mlp = sums[0] + got[0, 0, u].astype(F32) + got[1, 0, u].astype(F32)
        known = here[:, :, u * unit : (u + 1) * unit].astype(F32)
        mixed[u] = (known + mlp.reshape(n_x, block, unit)).astype(BF16)
        full[me.t, u, me.x] = mixed[u, me.x]
        for s, peer in enumerate(peers):
            at = (u, s)
            copy = push(mixed.at[u, me.x_at(s + 1)], full.at[me.t, u, me.x], swap_send.at[at], swap_recv.at[at], peer)
            copy.start()
            swaps.append(copy)

    for s in range(1, n_x):
        finals[s - 1].wait_recv()
        piece = fin.at[me.peer(n_x - s)]
        copy = push(piece, piece, twin_send.at[s], twin_recv.at[s], twin)
        copy.start()
        finals.append(copy)
    kin = []
    for s in range(1, n_x):
        rest_p[s - 1].wait_recv()
        piece = p_v.at[me.peer(n_x - s), second]
        copy = push(piece, piece, kin_send.at[s], kin_recv.at[s], twin)
        copy.start()
        kin.append(copy)

    def ring(k, d, u):
        t = me.at((1 - k) * (1 - 2 * d))
        view = full.at[t, u]
        if k == far:
            view = full.at[t, u, :, pl.ds(d * (block // 2), block // 2)]
        at = (d, k - 1, u)
        return push(view, view, ring_send.at[at], ring_recv.at[at], line[d])

    for u in range(CORES):
        for s in range(n_x - 1):
            swaps[u * (n_x - 1) + s].wait_recv()
        for d in range(2):
            ring(1, d, u).start()

    for copy in finals[n_x - 1 :]:
        copy.wait_recv()
    strip = min(256, tokens)

    @pl.loop(0, tokens // strip)
    def _(r):
        first = pl.multiple_of(r * strip, strip)
        places = me.dp * tokens + first + lax.broadcasted_iota(jnp.int32, (strip, tokens), 0)
        total = None
        for i in range(n_dp):
            pick = (places == dest[:, i * tokens : (i + 1) * tokens]).astype(F32).astype(BF16)
            piece = jnp.dot(pick, fin[i], preferred_element_type=F32)
            total = piece if total is None else total + piece
        target[pl.ds(first, strip), :] = total

    all_proj(lambda copy: copy.wait())
    for copy in kin:
        copy.wait_recv()
    p_tile = min(256, target.shape[1])

    def project(ts):
        @pl.loop(0, target.shape[1] // p_tile)
        def _(c):
            at = pl.ds(pl.multiple_of(c * p_tile, p_tile), p_tile)
            total = None
            for x in range(n_x):
                for u in range(CORES):
                    rows = jnp.concatenate([full[t, u, x] for t in ts], axis=0)
                    piece = jnp.dot(rows, p_v[x * CORES + u, :, at], preferred_element_type=F32)
                    total = piece if total is None else total + piece
            for i, t in enumerate(ts):
                rows = pl.ds(pl.multiple_of(t * block, block), block)
                gap = total[i * block : (i + 1) * block] - target[rows, at]
                residue[rows, at] = gap
                column[rows, :] = column[rows, :] + jnp.sum(gap * gap, axis=1, keepdims=True)

    project([me.t])
    for k in range(1, far + 1):
        for u in range(CORES):
            for d in range(2):
                ring(k, d, u).wait_recv()
                if k < far:
                    ring(k + 1, d, u).start()
        project([me.at(-k), me.at(k)] if k < far else [me.at(far)])

    row[...] = as_row(column[...])
    out_cols = out.shape[1]
    x = lax.div(me.t, per)
    u = lax.div(lax.rem(me.t, per) * out_cols, unit)
    inner = pl.multiple_of(lax.rem(me.t * out_cols, unit), out_cols)
    for t in range(n_t):
        out[t * block : (t + 1) * block, :] = full[t, u, x, :, pl.ds(inner, out_cols)]
    loss[...] = add_over(plane, row, rows_got, row_send, row_recv) / (n_t * target.shape[1])
    for u in range(CORES):
        for d in range(2):
            for k in range(1, far + 1):
                hop(k, d, u).wait_send()
                ring(k, d, u).wait_send()
    for copy in finals + swaps + rest_p + kin:
        copy.wait_send()


def student(final, dest_row, here, hiddens, w_down, downs, proj, projs):
    n_t, n_dp = lax.axis_size("tensor"), lax.axis_size("dp")
    n_x, far = n_dp // CORES, n_t // 2
    tokens, width = final.shape
    ff, unit = w_down.shape
    rows, cols = hiddens.shape[1:]
    block = tokens // n_t
    d_cols = CORES * unit * n_x // n_t
    sems = pltpu.SemaphoreType.DMA
    hops = (2, far, CORES)
    vmem = pltpu.VMEM
    return pl.pallas_call(
        student_kernel,
        out_shape=(
            jax.ShapeDtypeStruct((tokens, d_cols), BF16),
            jax.ShapeDtypeStruct((tokens, width), F32),
            jax.ShapeDtypeStruct((8, tokens), F32),
        ),
        in_specs=[VMEM] * 3 + [ANY] * 5,
        out_specs=(VMEM, VMEM, VMEM),
        scratch_shapes=[
            vmem((CORES, ff, unit), BF16),
            vmem((n_x, rows, cols), BF16),
            vmem((n_dp,) + proj.shape, BF16),
            vmem((n_dp, tokens, width), BF16),
            vmem((n_t, CORES, n_x, block, unit), BF16),
            vmem((CORES, n_x, block, unit), BF16),
            vmem(hops + (n_x * block, unit), BF16),
            vmem(hops + (n_x * block, unit), BF16),
            vmem((2, n_x * block, unit), F32),
            vmem((tokens, width), F32),
            vmem((tokens, 1), F32),
            vmem((8, tokens), F32),
            vmem((n_t - 1, 8, tokens), F32),
            sems((CORES,)),
            sems((n_x,)),
            sems((n_dp, 2)),
            sems(hops),
            sems(hops),
            sems((n_x,)),
            sems((n_x,)),
            sems((n_x,)),
            sems((n_x,)),
            sems((CORES, n_x)),
            sems((CORES, n_x)),
            sems(hops),
            sems(hops),
            sems((n_t - 1,)),
            sems((n_t - 1,)),
            sems((n_x,)),
            sems((n_x,)),
            sems((n_x,)),
            sems((n_x,)),
        ],
        compiler_params=pltpu.CompilerParams(collective_id=2, has_side_effects=True, vmem_limit_bytes=GRANT),
        name="student",
    )(final, dest_row[None, :], here, hiddens, w_down, downs, proj, projs)


def local(
    attn_ctx,
    w_out,
    resid,
    teacher_gain,
    dest_row,
    student_in,
    student_gain,
    w_gate,
    w_up,
    w_down,
    proj,
):
    final, hiddens, projs, downs, here = front(
        student_in, student_gain, attn_ctx, resid, teacher_gain, w_gate, w_up, w_down, w_out, proj
    )
    out, residue, loss = student(final, dest_row, here, hiddens, w_down, downs, proj, projs)
    return (out, loss[0], residue)


def solution(mesh):
    placed = (
        P("dp", "tensor"),
        P("tensor", None),
        P(("dp", "tensor"), None),
        P(),
        P(),
        P("dp", "tensor"),
        P(),
        P("dp", "tensor"),
        P("dp", "tensor"),
        P("tensor", "dp"),
        P("dp", "tensor"),
    )
    return jax.shard_map(
        local,
        mesh=mesh,
        in_specs=placed,
        out_specs=(P("dp", "tensor"), P("dp"), P("dp", "tensor")),
        check_vma=False,
    )
```

time: 336 us -> 290 us (0.86)
  Pallas kernels: 326 us -> 280 us
    pallas_call x3 -> x1, Pallas kernels: 225 us -> 177 us  [front(): pl.pallas_call(front_kernel, out_shape=(shape((tokens, width), BF16), sha...]
where the time goes in v1:
time: 290 us
  Pallas kernels  280 us (97%)
  local copies, waits for them, and re-layouts  8.98 us (3%)
    pallas_call x1, Pallas kernels, front(): pl.pallas_call(front_kernel, out_shape=(shape((tokens, width), BF16), sha...  177 us
    pallas_call x1, Pallas kernels, student(): pl.pallas_call(student_kernel, out_shape=(jax.ShapeDtypeStruct((tokens, d...  103 us

profile of v1, /device:TPU:0, one launch (start us, length us, event | category | flops | bytes accessed | tf_op | source)
XLA Modules:
  0.0 289.8 jit_solution(14051599102927540841)
XLA Ops:
  0.6 1.3 broadcast_in_dim.9.s_gain
  1.9 1.3 broadcast_in_dim.10.t_gain
  3.3 177.2 %front.1 = (bf16[512,1024]{1,0:T(8,128)(2,1)}, bf16[2,1024,896]{2,1,0:T(8,128)(2,1)}, bf16[4,1024,1024]{2,1,0:T(8,128)(2,1)}, bf16[1792,1024]{1,0:T(8,128)(2,1)}, bf16[2,64,2048]{2,1,0:T(8,128)(2,1)}) custom-call(bf16[512,512]{1,0:T(8,128)(2,1)} %rows_in.1, bf16[1,4096]{1,0:T(2,128)(2,1)} %broadcast_in_dim.9.s_gain, bf16[512,1024]{1,0:T(8,128)(2,1)} %ctx.1, ...), custom_call_target="tpu_custom_call" | custom-call | tf_op jit(solution)/shard_map/front/pallas_call | solution.py:382
  180.5 103.0 %student.1 = (bf16[512,512]{1,0:T(8,128)(2,1)}, f32[512,1024]{1,0:T(8,128)}, f32[8,512]{1,0:T(8,128)}) custom-call(bf16[512,1024]{1,0:T(8,128)(2,1)} %get-tuple-element.11.final, s32[1,2048]{1,0:T(1,128)} %bitcast.2, bf16[2,64,2048]{2,1,0:T(8,128)(2,1)} %get-tuple-element.12.here, bf16[2,1024,896]{2,1,0:T(8,128)(2,1)} %get-tuple-element.13.hiddens, ...), custom_call_target="tpu_custom_call" | custom-call | tf_op jit(solution)/shard_map/student/pallas_call | solution.py:668
  283.5 1.3 slice.3
  284.8 1.9 copy.16
  286.6 3.2 %copy.17 = f32[512,1024]{1,0:T(8,128)} copy(f32[512,1024]{1,0:T(8,128)} %get-tuple-element.24) | data formatting | bytes 4194304

commit v2 on v1

--- a/solution.py
+++ b/solution.py
@@ -94,10 +94,14 @@
     return jnp.transpose(jnp.broadcast_to(row[:1], (128, row.shape[1])))[:, :1]
 
 
-def add_over(peers, own, got, send, recv):
+def spread(peers, own, got, send, recv):
     copies = [push(own, got.at[k], send.at[k], recv.at[k], peer) for k, peer in enumerate(peers)]
     for copy in copies:
         copy.start()
+    return copies
+
+
+def add_up(copies, own, got):
     total = own[...]
     for k, copy in enumerate(copies):
         copy.wait_recv()
@@ -111,12 +115,12 @@
 
 
 def front_kernel(
-    rows_in, s_gain, ctx, resid, t_gain, gate, up, down, w_out, proj,
+    rows_in, s_gain, ctx, resid, gate, up, down, w_out, proj,
     out, hiddens, projs, downs, here,
     x_v, g_v, u_v, g_sum, u_sum, squares, hid_v,
-    w_v, sums, sent, got, total, row, rows_got,
-    own_sem, ring_send, ring_recv, x_send, x_recv, core_send, core_recv,
-    hid_send, hid_recv, w_sem, send, recv, row_send, row_recv,
+    w_v, sums, sent, got, total,
+    own_sem, out_sem, ring_send, ring_recv, x_send, x_recv, core_send, core_recv,
+    hid_send, hid_recv, w_sem, send, recv,
 ):
     me = Place()
     n_x, n_t, n_dp, far = me.n_x, me.n_t, me.n_dp, me.far
@@ -128,7 +132,6 @@
     line = [(me.dp, me.at(1)), (me.dp, me.at(-1))]
     peers = [(me.peer(s), me.t) for s in range(1, n_x)]
     twin = (me.sibling, me.t)
-    plane = [(me.dp, lax.rem(me.t + k, n_t)) for k in range(1, n_t)]
 
     order = [far]
     for k in range(far - 1, 0, -1):
@@ -145,7 +148,7 @@
         if after < len(order):
             load(order[after]).start()
 
-    greet(plane + peers + [twin])
+    greet(line + peers + [twin])
     started = []
 
     def start(copy):
@@ -177,7 +180,7 @@
                 push(part_of(w, me.x_at(s + 1), cols), buf.at[me.dp], x_send.at[i, s], x_recv.at[i, s], peer)
             )
     for s, peer in enumerate(peers):
-        first = pl.ds(0, proj.shape[0] // 2)
+        first = pl.ds(0, proj.shape[0] * 3 // 4)
         moved[3, s] = start(
             push(proj.at[first], projs.at[me.dp, first], x_send.at[3, s], x_recv.at[3, s], peer)
         )
@@ -204,7 +207,7 @@
             moved[i, s - 1].wait_recv()
             block = buf.at[me.peer(n_x - s)]
             if i == 3:
-                block = buf.at[me.peer(n_x - s), pl.ds(0, proj.shape[0] // 2)]
+                block = buf.at[me.peer(n_x - s), pl.ds(0, proj.shape[0] * 3 // 4)]
             at = (i if i == 3 else i - 1, s)
             copies.append(start(push(block, block, core_send.at[at], core_recv.at[at], twin)))
 
@@ -340,15 +343,13 @@
         term(0, i)
         for d in range(2):
             hop(1, d, i).wait_recv()
-        total[i * half : (i + 1) * half, :] = (
-            sums[...] + got[0, 0, i].astype(F32) + got[1, 0, i].astype(F32)
-        )
-    row[...] = as_row(jnp.sum(total[...] * total[...], axis=1, keepdims=True))
-    relay(3, projs, late)
-    sums_of = add_over(plane, row, rows_got, row_send, row_recv)
-    scale = as_column(lax.rsqrt(sums_of / (n_t * width) + 1e-06))
-    weight = t_gain[:, pl.ds(pl.multiple_of(me.t * width, width), width)].astype(F32)
-    out[...] = (total[...] * scale * weight).astype(BF16)
+        at = pl.ds(i * half, half)
+        total[at, :] = sums[...] + got[0, 0, i].astype(F32) + got[1, 0, i].astype(F32)
+        copy = pltpu.make_async_copy(total.at[at], out.at[at], out_sem.at[i])
+        copy.start()
+        hid.append(copy)
+        if i == 0:
+            relay(3, projs, late)
     for copy in late:
         copy.wait_recv()
     for r in range(strips):
@@ -366,7 +367,7 @@
                 hop(k, d, u).wait_send()
 
 
-def front(student_in, student_gain, attn_ctx, resid, teacher_gain, w_gate, w_up, w_down, w_out, proj):
+def front(student_in, student_gain, attn_ctx, resid, w_gate, w_up, w_down, w_out, proj):
     n_t, n_dp = lax.axis_size("tensor"), lax.axis_size("dp")
     n_x, far = n_dp // CORES, n_t // 2
     tokens, d_cols = student_in.shape
@@ -382,14 +383,14 @@
     return pl.pallas_call(
         front_kernel,
         out_shape=(
-            shape((tokens, width), BF16),
+            shape((tokens, width), F32),
             shape((n_x, n_x * tokens, cols), BF16),
             shape((n_dp,) + proj.shape, BF16),
             shape(w_down.shape, BF16),
             shape((n_x, block, per * d_cols), BF16),
         ),
-        in_specs=[VMEM] * 5 + [ANY] * 5,
-        out_specs=(VMEM, ANY, ANY, ANY, ANY),
+        in_specs=[VMEM] * 4 + [ANY] * 5,
+        out_specs=(ANY,) * 5,
         scratch_shapes=[
             vmem((n_t, n_x, tokens, d_cols), BF16),
             vmem((n_dp, depth, cols), BF16),
@@ -403,9 +404,8 @@
             vmem(units + (tokens // 2, width), BF16),
             vmem(units + (tokens // 2, width), BF16),
             vmem((tokens, width), F32),
-            vmem((8, tokens), F32),
-            vmem((n_t - 1, 8, tokens), F32),
             sems((3 + n_x * per,)),
+            sems((2,)),
             sems((2, far, n_x)),
             sems((2, far, n_x)),
             sems((4, n_x)),
@@ -417,22 +417,21 @@
             sems((SLOTS,)),
             sems(units),
             sems(units),
-            sems((n_t - 1,)),
-            sems((n_t - 1,)),
         ],
         compiler_params=pltpu.CompilerParams(collective_id=0, has_side_effects=True, vmem_limit_bytes=GRANT),
         name="front",
     )(
-        student_in, student_gain[None, :], attn_ctx, resid, teacher_gain[None, :],
+        student_in, student_gain[None, :], attn_ctx, resid,
         column_part(w_gate, n_x), column_part(w_up, n_x), w_down, w_out, proj,
     )
 
 
 def student_kernel(
-    final, dest, here, hiddens, w_down, downs, proj, projs, out, residue, loss,
-    d_v, h_v, p_v, fin, full, mixed, sent, got, sums, target, column, row, rows_got,
+    t_gain, dest, here, raw, hiddens, w_down, downs, proj, projs, out, residue, loss,
+    raw_v, final, squares, squares_got, d_v, h_v, p_v, fin, full, mixed, sent, got, sums, target, column, row, rows_got,
     d_sem, h_sem, p_sem, send, recv, fin_send, fin_recv, twin_send, twin_recv,
     swap_send, swap_recv, ring_send, ring_recv, row_send, row_recv, rest_send, rest_recv, kin_send, kin_recv,
+    raw_sem, square_send, square_recv,
 ):
     me = Place()
     n_x, n_t, n_dp, far = me.n_x, me.n_t, me.n_dp, me.far
@@ -455,28 +454,28 @@
         def _():
             pltpu.make_async_copy(other, dst, sem).start()
 
+    raw_copy = pltpu.make_async_copy(raw, raw_v, raw_sem)
+    raw_copy.start()
     for x in range(n_x):
         pltpu.make_async_copy(hiddens.at[x], h_v.at[x], h_sem.at[x]).start()
-    for u in range(CORES):
-        either(me.core, u, w_down, downs, d_v.at[u], d_sem.at[u])
+    either(me.core, 0, w_down, downs, d_v.at[0], d_sem.at[0])
     greet(plane + peers + [twin])
-    finals = [
-        push(final, fin.at[me.dp], fin_send.at[s], fin_recv.at[s], peer) for s, peer in enumerate(peers)
-    ] + [push(final, fin.at[me.dp], twin_send.at[0], twin_recv.at[0], twin)]
-    for copy in finals:
-        copy.start()
-    p_half = proj.shape[0] // 2
-    second = pl.ds(p_half, p_half)
+    p_first = proj.shape[0] * 3 // 4
+    second = pl.ds(p_first, proj.shape[0] - p_first)
     rest_p = [
         push(proj.at[second], p_v.at[me.dp, second], rest_send.at[s], rest_recv.at[s], peer)
         for s, peer in enumerate(peers)
     ]
     for copy in rest_p:
         copy.start()
-    fin[me.dp] = final[...]
-    column[...] = jnp.zeros_like(column)
+    raw_copy.wait()
+    squares[...] = as_row(jnp.sum(raw_v[...] * raw_v[...], axis=1, keepdims=True))
+    shared = spread(plane, squares, squares_got, square_send, square_recv)
     for x in range(n_x):
         pltpu.make_async_copy(hiddens.at[x], h_v.at[x], h_sem.at[x]).wait()
+    for u in range(1, CORES):
+        either(me.core, u, w_down, downs, d_v.at[u], d_sem.at[u])
+    column[...] = jnp.zeros_like(column)
 
     tile = min(256, unit)
 
@@ -509,7 +508,28 @@
             src, dst = src.at[pl.ds(d * half, half)], dst.at[pl.ds(d * half, half)]
         return push(src, dst, send.at[at], recv.at[at], line[d])
 
-    for u in range(CORES):
+    def of_proj(i, j, act):
+        at = second if j else pl.ds(0, p_first)
+
+        @pl.when(me.dp == i)
+        def _():
+            act(pltpu.make_async_copy(proj.at[at], p_v.at[i, at], p_sem.at[i, j]))
+
+        @pl.when(me.dp != i)
+        def _():
+            act(pltpu.make_async_copy(projs.at[i, at], p_v.at[i, at], p_sem.at[i, j]))
+
+    def all_proj(act):
+        for i in range(n_dp):
+            of_proj(i, 0, act)
+
+            @pl.when(me.x == i // CORES)
+            def _():
+                of_proj(i, 1, act)
+
+    swaps = {}
+
+    def first_hop(u):
         pltpu.make_async_copy(w_down, d_v.at[u], d_sem.at[u]).wait()
         term([far], u)
         for d in range(2):
@@ -517,40 +537,19 @@
             sent[d, far - 1, u, rows] = sums[0, rows].astype(BF16)
             hop(far, d, u).start()
 
-    def of_proj(i, j, act):
-        at = pl.ds(j * p_half, p_half)
-
-        @pl.when(me.dp == i)
-        def _():
-            act(pltpu.make_async_copy(proj.at[at], p_v.at[i, at], p_sem.at[i, j]))
-
-        @pl.when(me.dp != i)
-        def _():
-            act(pltpu.make_async_copy(projs.at[i, at], p_v.at[i, at], p_sem.at[i, j]))
-
-    def all_proj(act):
-        for i in range(n_dp):
-            of_proj(i, 0, act)
-
-            @pl.when(me.x == i // CORES)
-            def _():
-                of_proj(i, 1, act)
-
-    all_proj(lambda copy: copy.start())
-    for k in range(far - 1, 0, -1):
-        for u in range(CORES):
-            term([k, -k], u)
-            for d in range(2):
-                hop(k + 1, d, u).wait_recv()
-                if k + 1 == far:
-                    rows, rest = (slice(d * half, (d + 1) * half), slice((1 - d) * half, (2 - d) * half))
-                    sent[d, k - 1, u, rows] = (sums[d, rows] + got[d, k, u, rows].astype(F32)).astype(BF16)
-                    sent[d, k - 1, u, rest] = sums[d, rest].astype(BF16)
-                else:
-                    sent[d, k - 1, u] = (sums[d] + got[d, k, u].astype(F32)).astype(BF16)
-                hop(k, d, u).start()
-    swaps = []
-    for u in range(CORES):
+    def next_hop(k, u):
+        term([k, -k], u)
+        for d in range(2):
+            hop(k + 1, d, u).wait_recv()
+            if k + 1 == far:
+                rows, rest = (slice(d * half, (d + 1) * half), slice((1 - d) * half, (2 - d) * half))
+                sent[d, k - 1, u, rows] = (sums[d, rows] + got[d, k, u, rows].astype(F32)).astype(BF16)
+                sent[d, k - 1, u, rest] = sums[d, rest].astype(BF16)
+            else:
+                sent[d, k - 1, u] = (sums[d] + got[d, k, u].astype(F32)).astype(BF16)
+            hop(k, d, u).start()
+
+    def last_hop(u):
         term([0], u)
         for d in range(2):
             hop(1, d, u).wait_recv()
@@ -560,23 +559,10 @@
         full[me.t, u, me.x] = mixed[u, me.x]
         for s, peer in enumerate(peers):
             at = (u, s)
-            copy = push(mixed.at[u, me.x_at(s + 1)], full.at[me.t, u, me.x], swap_send.at[at], swap_recv.at[at], peer)
-            copy.start()
-            swaps.append(copy)
-
-    for s in range(1, n_x):
-        finals[s - 1].wait_recv()
-        piece = fin.at[me.peer(n_x - s)]
-        copy = push(piece, piece, twin_send.at[s], twin_recv.at[s], twin)
-        copy.start()
-        finals.append(copy)
-    kin = []
-    for s in range(1, n_x):
-        rest_p[s - 1].wait_recv()
-        piece = p_v.at[me.peer(n_x - s), second]
-        copy = push(piece, piece, kin_send.at[s], kin_recv.at[s], twin)
-        copy.start()
-        kin.append(copy)
+            swaps[at] = push(
+                mixed.at[u, me.x_at(s + 1)], full.at[me.t, u, me.x], swap_send.at[at], swap_recv.at[at], peer
+            )
+            swaps[at].start()
 
     def ring(k, d, u):
         t = me.at((1 - k) * (1 - 2 * d))
@@ -586,11 +572,52 @@
         at = (d, k - 1, u)
         return push(view, view, ring_send.at[at], ring_recv.at[at], line[d])
 
-    for u in range(CORES):
+    def gather(u):
         for s in range(n_x - 1):
-            swaps[u * (n_x - 1) + s].wait_recv()
+            swaps[u, s].wait_recv()
         for d in range(2):
             ring(1, d, u).start()
+
+    finals = []
+    for stage in range(far + 2):
+        for u in range(CORES):
+            k = far - stage + u
+            if k == far:
+                first_hop(u)
+            elif 0 < k < far:
+                next_hop(k, u)
+            elif k == 0:
+                last_hop(u)
+            if stage == 1 and u == 0:
+                all_proj(lambda copy: copy.start())
+            if stage == far and u == 1:
+                gather(0)
+        if stage == 1:
+            scale = as_column(lax.rsqrt(add_up(shared, squares, squares_got) / (n_t * target.shape[1]) + 1e-06))
+            width = target.shape[1]
+            weight = t_gain[:, pl.ds(pl.multiple_of(me.t * width, width), width)].astype(F32)
+            final[...] = (raw_v[...] * scale * weight).astype(BF16)
+            fin[me.dp] = final[...]
+            finals += [
+                push(final, fin.at[me.dp], fin_send.at[s], fin_recv.at[s], peer) for s, peer in enumerate(peers)
+            ] + [push(final, fin.at[me.dp], twin_send.at[0], twin_recv.at[0], twin)]
+            for copy in finals:
+                copy.start()
+    gather(1)
+
+    for s in range(1, n_x):
+        finals[s - 1].wait_recv()
+        piece = fin.at[me.peer(n_x - s)]
+        copy = push(piece, piece, twin_send.at[s], twin_recv.at[s], twin)
+        copy.start()
+        finals.append(copy)
+    kin = []
+    for s in range(1, n_x):
+        rest_p[s - 1].wait_recv()
+        piece = p_v.at[me.peer(n_x - s), second]
+        copy = push(piece, piece, kin_send.at[s], kin_recv.at[s], twin)
+        copy.start()
+        kin.append(copy)
 
     for copy in finals[n_x - 1 :]:
         copy.wait_recv()
@@ -644,20 +671,20 @@
     inner = pl.multiple_of(lax.rem(me.t * out_cols, unit), out_cols)
     for t in range(n_t):
         out[t * block : (t + 1) * block, :] = full[t, u, x, :, pl.ds(inner, out_cols)]
-    loss[...] = add_over(plane, row, rows_got, row_send, row_recv) / (n_t * target.shape[1])
+    loss[...] = add_up(spread(plane, row, rows_got, row_send, row_recv), row, rows_got) / (n_t * target.shape[1])
     for u in range(CORES):
         for d in range(2):
             for k in range(1, far + 1):
                 hop(k, d, u).wait_send()
                 ring(k, d, u).wait_send()
-    for copy in finals + swaps + rest_p + kin:
+    for copy in finals + list(swaps.values()) + rest_p + kin:
         copy.wait_send()
 
 
-def student(final, dest_row, here, hiddens, w_down, downs, proj, projs):
+def student(raw, teacher_gain, dest_row, here, hiddens, w_down, downs, proj, projs):
     n_t, n_dp = lax.axis_size("tensor"), lax.axis_size("dp")
     n_x, far = n_dp // CORES, n_t // 2
-    tokens, width = final.shape
+    tokens, width = raw.shape
     ff, unit = w_down.shape
     rows, cols = hiddens.shape[1:]
     block = tokens // n_t
@@ -672,9 +699,13 @@
             jax.ShapeDtypeStruct((tokens, width), F32),
             jax.ShapeDtypeStruct((8, tokens), F32),
         ),
-        in_specs=[VMEM] * 3 + [ANY] * 5,
+        in_specs=[VMEM] * 3 + [ANY] * 6,
         out_specs=(VMEM, VMEM, VMEM),
         scratch_shapes=[
+            vmem((tokens, width), F32),
+            vmem((tokens, width), BF16),
+            vmem((8, tokens), F32),
+            vmem((n_t - 1, 8, tokens), F32),
             vmem((CORES, ff, unit), BF16),
             vmem((n_x, rows, cols), BF16),
             vmem((n_dp,) + proj.shape, BF16),
@@ -707,10 +738,13 @@
             sems((n_x,)),
             sems((n_x,)),
             sems((n_x,)),
+            sems(()),
+            sems((n_t - 1,)),
+            sems((n_t - 1,)),
         ],
         compiler_params=pltpu.CompilerParams(collective_id=2, has_side_effects=True, vmem_limit_bytes=GRANT),
         name="student",
-    )(final, dest_row[None, :], here, hiddens, w_down, downs, proj, projs)
+    )(teacher_gain[None, :], dest_row[None, :], here, raw, hiddens, w_down, downs, proj, projs)
 
 
 def local(
@@ -726,10 +760,10 @@
     w_down,
     proj,
 ):
-    final, hiddens, projs, downs, here = front(
-        student_in, student_gain, attn_ctx, resid, teacher_gain, w_gate, w_up, w_down, w_out, proj
+    raw, hiddens, projs, downs, here = front(
+        student_in, student_gain, attn_ctx, resid, w_gate, w_up, w_down, w_out, proj
     )
-    out, residue, loss = student(final, dest_row, here, hiddens, w_down, downs, proj, projs)
+    out, residue, loss = student(raw, teacher_gain, dest_row, here, hiddens, w_down, downs, proj, projs)
     return (out, loss[0], residue)
 
 

time: 290 us -> 282 us (0.972)
  Pallas kernels: 280 us -> 272 us
    pallas_call x1, Pallas kernels: 177 us -> 171 us  [front(): pl.pallas_call(front_kernel, out_shape=(shape((tokens, width), F32), shap...]
where the time goes in v2:
time: 282 us; the launch traced here: 281 us
  Pallas kernels  272 us (96%)
  local copies, waits for them, and re-layouts  8.99 us (3%)
    pallas_call x1, Pallas kernels, front(): pl.pallas_call(front_kernel, out_shape=(shape((tokens, width), F32), shap...  171 us
    pallas_call x1, Pallas kernels, student(): pl.pallas_call(student_kernel, out_shape=(jax.ShapeDtypeStruct((tokens, d...  101 us

profile of v2, /device:TPU:0, one launch (start us, length us, event | category | flops | bytes accessed | tf_op | source)
XLA Modules:
  0.0 281.2 jit_solution(15387095081188724586)
XLA Ops:
  0.6 1.3 broadcast_in_dim.11.s_gain
  1.9 1.3 broadcast_in_dim.9.t_gain
  3.3 170.9 %front.1 = (f32[512,1024]{1,0:T(8,128)}, bf16[2,1024,896]{2,1,0:T(8,128)(2,1)}, bf16[4,1024,1024]{2,1,0:T(8,128)(2,1)}, bf16[1792,1024]{1,0:T(8,128)(2,1)}, bf16[2,64,2048]{2,1,0:T(8,128)(2,1)}) custom-call(bf16[512,512]{1,0:T(8,128)(2,1)} %rows_in.1, bf16[1,4096]{1,0:T(2,128)(2,1)} %broadcast_in_dim.11.s_gain, bf16[512,1024]{1,0:T(8,128)(2,1)} %ctx.1, ...), custom_call_target="tpu_custom_call" | custom-call | tf_op jit(solution)/shard_map/front/pallas_call | solution.py:383
  174.2 100.6 %student.1 = (bf16[512,512]{1,0:T(8,128)(2,1)}, f32[512,1024]{1,0:T(8,128)}, f32[8,512]{1,0:T(8,128)}) custom-call(bf16[1,8192]{1,0:T(2,128)(2,1)} %broadcast_in_dim.9.t_gain, s32[1,2048]{1,0:T(1,128)} %bitcast.2, bf16[2,64,2048]{2,1,0:T(8,128)(2,1)} %get-tuple-element.11.here, f32[512,1024]{1,0:T(8,128)} %get-tuple-element.12.raw, ...), custom_call_target="tpu_custom_call" | custom-call | tf_op jit(solution)/shard_map/student/pallas_call | solution.py:695
  274.9 1.3 slice.3
  276.2 1.9 copy.16
  278.0 3.2 %copy.17 = f32[512,1024]{1,0:T(8,128)} copy(f32[512,1024]{1,0:T(8,128)} %get-tuple-element.24) | data formatting | bytes 4194304
